TPU v7x, 128 devices: a whole 4x4x4 slice. The times are simulated.
128 devices in a mesh: fsdp: 8 (over z_hi, y), tp: 16 (over z_lo, x, core).
Axes of the slice: x: 4, y: 4, z: 4 (z_hi: 2, z_lo: 2; z = z_hi * 2 + z_lo), core: 2. Of those that a mesh axis runs over, the one named last changes fastest.
Arguments:
- tokens: bfloat16 [2048, 8192], P('fsdp', 'tp'), may hold values from -6 to 6
- out_grad: bfloat16 [2048, 8192], P('fsdp', 'tp'), may hold values from -6 to 6
- gate_weight: bfloat16 [8192, 2048], P('fsdp', 'tp'), may hold values from -0.0625 to 0.0625
- up_weight: bfloat16 [8192, 2048], P('fsdp', 'tp'), may hold values from -0.0625 to 0.0625
- down_weight: bfloat16 [2048, 8192], P('tp', 'fsdp'), may hold values from -0.125 to 0.125
Outputs:
- input_grad: bfloat16 [2048, 8192], P('fsdp', 'tp')
- gate_grad: float32 [8192, 2048], P('fsdp', 'tp')
- up_grad: float32 [8192, 2048], P('fsdp', 'tp')
- down_grad: float32 [2048, 8192], P('tp', 'fsdp')
All inputs are finite; a program needn't handle non-finite values.
Results may differ from a plain program's by a relative error of at most 0.0023.
Values may be sent and summed in bfloat16 or wider, within the bound.
No kernel may reach another device: no remote copies, remote signals or barrier semaphores. Data moves between devices by JAX's collectives and lax.ppermute only.
A program may use at most 128 MiB of HBM per device.

v0:
```python
import math
import jax
import jax.numpy as jnp
from jax import lax
from jax.sharding import Mesh
from jax.sharding import PartitionSpec as P

FSDP = ("fsdp_0", "fsdp_1")


def laid_out(parts, dim):
    parts = jnp.moveaxis(parts, 0, dim)
    dims = parts.shape
    return parts.reshape(*dims[:dim], dims[dim] * dims[dim + 1], *dims[dim + 2 :])


def one_gather(arrays, axis, dims):
    line = jnp.concatenate([a.reshape(-1) for a in arrays])
    lines, at, outs = (lax.all_gather(line, axis), 0, [])
    for a, dim in zip(arrays, dims):
        parts = lines[:, at : at + a.size].reshape(-1, *a.shape)
        outs.append(laid_out(parts, dim))
        at += a.size
    return tuple(outs)


def stacked_from(value, axes, turns):
    parts = value[None]
    for k in turns:
        parts = lax.all_gather(parts, axes[k], axis=0, tiled=True)
    current = [lax.axis_size(axes[k]) for k in reversed(turns)]
    parts = parts.reshape(*current, *value.shape)
    turned = sorted(range(len(turns)), key=lambda place: turns[len(turns) - 1 - place])
    return parts.transpose(*turned, *range(len(turns), parts.ndim)).reshape(-1, *value.shape)


def gathered_by_axis(value, axes, turns, dim):
    return laid_out(stacked_from(value, axes, turns), dim)


def taken_in(value, axes, turns, dim, absorb, carry):
    everything = jax.tree.map(lambda part: gathered_by_axis(part, axes, turns, dim), value)
    return absorb(carry, everything, jnp.int32(0))


def own_rows(portion, rows, axis):
    count = rows * lax.axis_size(axis)
    return lax.psum_scatter(portion(jnp.int32(0), count), axis, scatter_dimension=0, tiled=True)


def column_term(left, right, start, count, factor):
    block = lax.dynamic_slice_in_dim(left, start, count, 1)
    product = lax.dot_general(
        block, right, (((0,), (0,)), ((), ())), preferred_element_type=jnp.float32
    )
    return product * factor


def shards(tokens, out_grad, gate_weight, up_weight, down_weight):
    factor = 1.0 / math.sqrt(tokens.shape[0] * lax.axis_size(FSDP))
    whole = lax.all_gather(tokens, "tp", axis=1, tiled=True)
    grads = lax.all_gather(out_grad, "tp", axis=1, tiled=True)
    gate_full, up_full = one_gather((gate_weight, up_weight), FSDP, (0, 0))
    gate = jnp.dot(whole, gate_full, preferred_element_type=jnp.float32)
    up = jnp.dot(whole, up_full, preferred_element_type=jnp.float32)

    def add_down(total, piece, start):
        columns = lax.dynamic_slice_in_dim(grads, start, piece.shape[1], 1)
        return total + lax.dot_general(
            columns, piece, (((1,), (1,)), ((), ())), preferred_element_type=jnp.float32
        )

    initial = jnp.zeros((whole.shape[0], down_weight.shape[0]), jnp.float32)
    hidden_grad = taken_in(down_weight, FSDP, (0, 1), 1, add_down, initial)
    squashed = jax.nn.sigmoid(gate)
    activated = gate * squashed
    slope = squashed * (1.0 + gate * (1.0 - squashed))
    hidden = (activated * up).astype(jnp.bfloat16)
    gate_delta = (hidden_grad * up * slope).astype(jnp.bfloat16)
    up_delta = (hidden_grad * activated).astype(jnp.bfloat16)

    def rows_term(start, count):
        gate_rows = lax.dynamic_slice_in_dim(gate_full, start, count, 0)
        up_rows = lax.dynamic_slice_in_dim(up_full, start, count, 0)
        first = lax.dot_general(
            gate_rows, gate_delta, (((1,), (1,)), ((), ())), preferred_element_type=jnp.float32
        )
        second = lax.dot_general(
            up_rows, up_delta, (((1,), (1,)), ((), ())), preferred_element_type=jnp.float32
        )
        return first + second

    local_rows = own_rows(rows_term, tokens.shape[1], "tp")
    input_grad = local_rows.T.astype(jnp.bfloat16)
    rows_here = gate_weight.shape[0]

    def joint_term(start, count):
        return jnp.concatenate(
            [
                column_term(whole, gate_delta, start, count, factor),
                column_term(whole, up_delta, start, count, factor),
                column_term(grads, hidden, start, count, factor),
            ],
            axis=1,
        )

    summed = own_rows(joint_term, rows_here, FSDP)
    width = gate_delta.shape[1]
    gate_grad = summed[:, :width]
    up_grad = summed[:, width : 2 * width]
    down_grad = summed[:, 2 * width :].T
    return (input_grad, gate_grad, up_grad, down_grad)


def solution(mesh):
    finer = Mesh(mesh.devices.reshape(2, 4, mesh.shape["tp"]), ("fsdp_0", "fsdp_1", "tp"))
    return jax.shard_map(
        shards,
        mesh=finer,
        in_specs=(P(FSDP, "tp"), P(FSDP, "tp"), P(FSDP, "tp"), P(FSDP, "tp"), P("tp", FSDP)),
        out_specs=(P(FSDP, "tp"), P(FSDP, "tp"), P(FSDP, "tp"), P("tp", FSDP)),
        check_vma=False,
    )
```

profile of v0, /device:TPU:0, one launch (start us, length us, event | category | flops | bytes accessed | tf_op | source)
XLA Modules:
  0.0 450.9 jit_solution(1478735136044264735)
XLA Ops:
  7.2 0.0 all-gather.9.cloned.1.call-start
  7.2 12.9 %all-gather.1 = bf16[256,1024]{1,0:T(8,128)(2,1)} all-gather(bf16[128,1024]{1,0:T(8,128)(2,1)} %param.9), channel_id=3, replica_groups=mesh['fsdp_0'=2,'fsdp_1'=4,'tp'=16] {'fsdp_0'}, dimensions={0}, use_global_device_ids=true | all-gather | bytes 786432 | tf_op jit(solution)/shard_map/all_gather | solution.py:30
  20.1 0.0 all-gather.9.cloned.1.call-update
  20.2 0.0 all-gather.13.cloned.1.call-start
  20.2 1.9 pad_maximum_fusion.1
  22.1 0.0 all-gather.13.cloned.1.call-update
  22.1 0.0 all-gather.11.cloned.1.call-start
  22.1 0.7 all-gather.11.cloned.1.call-update
  22.8 0.0 all-gather.7.cloned.1.call-start
  22.9 0.5 all-gather.7.cloned.1.call-update
  23.4 0.0 reduce-scatter.3.cloned.1.call-start
  23.5 27.7 %all-gather.9.cloned.1.call-done = bf16[8,128,1024]{2,1,0:T(8,128)(2,1)} async-done(((bf16[2,128,1024]{2,1,0:T(8,128)(2,1)}), bf16[8,128,1024]{2,1,0:T(8,128)(2,1)}) %all-gather.9.cloned.1.call-update) | async-done | bytes 2097168 | tf_op jit(solution)/shard_map/all_gather | solution.py:30
  51.2 1.9 copy.27
  53.1 2.4 copy.28
  55.5 70.3 %all-gather.13.cloned.1.call-done = bf16[2097152]{0:T(1024)(128)(2,1)} async-done(((bf16[262144]{0:T(1024)(128)(2,1)}), bf16[2097152]{0:T(1024)(128)(2,1)}) %all-gather.13.cloned.1.call-update) | async-done | bytes 4194320 | tf_op jit(solution)/shard_map/all_gather | solution.py:19
  125.8 5.9 %reshape.28 = bf16[8,262144]{1,0:T(8,128)(2,1)} reshape(bf16[2097152]{0:T(1024)(128)(2,1)} %all-gather.13.cloned.1.call-done) | data formatting | bytes 8388608 | tf_op jit(solution)/shard_map/all_gather | solution.py:19
  131.7 3.9 fusion.6
  135.6 2.3 reshape_reshape.6
  137.9 2.6 reshape_reshape.7
  140.4 21.9 %all-gather.11.cloned.1.call-done = bf16[256,8192]{1,0:T(8,128)(2,1)} async-done(((bf16[256,512]{1,0:T(8,128)(2,1)}), bf16[256,8192]{1,0:T(8,128)(2,1)}) %all-gather.11.cloned.1.call-update) | async-done | bytes 4194320 | tf_op jit(solution)/shard_map/all_gather | solution.py:61
  162.3 0.0 copy-start
  162.3 4.2 convolution_bitcast_fusion
  166.6 0.0 copy-done
  166.6 1.3 convolution_bitcast_fusion.1
  167.9 33.2 %all-gather.7.cloned.1.call-done = bf16[256,8192]{1,0:T(8,128)(2,1)} async-done(((bf16[256,512]{1,0:T(8,128)(2,1)}), bf16[256,8192]{1,0:T(8,128)(2,1)}) %all-gather.7.cloned.1.call-update) | async-done | bytes 4194320 | tf_op jit(solution)/shard_map/all_gather | solution.py:62
  201.1 0.0 copy-start.2
  201.1 4.2 multiply_convert_fusion.1
  205.4 0.0 copy-done.2
  205.4 1.3 fusion.7
  206.6 4.5 convolution_add_fusion
  211.1 0.0 reduce-scatter.3.cloned.1.call-update
  211.2 0.2 reduce-scatter.5.cloned.1.call-start
  211.4 0.0 copy-start.1
  211.4 3.3 fusion.1
  214.7 0.2 copy-done.1
  214.8 0.0 copy-start.3
  214.8 0.9 fusion.2
  215.8 1.3 copy-done.3
  217.0 1.0 fusion
  218.0 5.0 %pad_maximum_fusion = f32[8192,384]{0,1:T(8,128)} fusion(f32[8192,128]{0,1:T(8,128)S(1)} %fusion, f32[8192,128]{0,1:T(8,128)S(1)} %fusion.1, f32[8192,128]{0,1:T(8,128)S(1)} %fusion.2), kind=kLoop, calls=%fused_computation | loop fusion | flops 6291456 | bytes 25165824 | tf_op jit(solution)/shard_map/concatenate | solution.py:98
  223.0 0.0 reduce-scatter.5.cloned.1.call-update
  223.0 63.3 %reduce-scatter.3.cloned.1.call-done = f32[512,256]{1,0:T(8,128)} async-done(((f32[8192,256]{1,0:T(8,128)}), f32[512,256]{1,0:T(8,128)}) %reduce-scatter.3.cloned.1.call-update) | async-done | bytes 524304 | tf_op jit(solution)/shard_map/reduce_scatter | solution.py:48
  286.3 1.1 convert_bitcast_fusion
  287.4 0.8 copy.31
  288.2 151.6 %reduce-scatter.5.cloned.1.call-done = f32[1024,384]{0,1:T(8,128)} async-done(((f32[8192,384]{0,1:T(8,128)}), f32[1024,384]{0,1:T(8,128)}) %reduce-scatter.5.cloned.1.call-update) | async-done | bytes 1572880 | tf_op jit(solution)/shard_map/reduce_scatter | solution.py:48
  439.8 2.3 slice_bitcast_fusion
  442.1 1.0 copy.32
  443.1 1.0 copy.33
Async XLA Ops:
  7.2 44.0 %all-gather.9.cloned.1.call-start = ((), (), s32[]{:S(2)}) async-start(), calls=%async_computation.3 | async-start | bytes 2621440 | tf_op jit(solution)/shard_map/all_gather | solution.py:30
  20.2 105.7 %all-gather.13.cloned.1.call-start = ((), (), s32[]{:S(2)}) async-start(), calls=%async_computation.7 | async-start | bytes 4718592 | tf_op jit(solution)/shard_map/all_gather | solution.py:19
  22.1 140.2 %all-gather.11.cloned.1.call-start = ((), (), s32[]{:S(2)}) async-start(), calls=%async_computation.4 | async-start | bytes 4456448 | tf_op jit(solution)/shard_map/all_gather | solution.py:61
  22.8 178.3 %all-gather.7.cloned.1.call-start = ((), (), s32[]{:S(2)}) async-start(), calls=%async_computation.2 | async-start | bytes 4456448 | tf_op jit(solution)/shard_map/all_gather | solution.py:62
  23.4 262.9 %reduce-scatter.3.cloned.1.call-start = ((), (), s32[]{:S(2)}) async-start(), calls=%async_computation.5 | async-start | bytes 8912896 | tf_op jit(solution)/shard_map/reduce_scatter | solution.py:48
  162.3 4.2 copy-start
  201.1 4.3 copy-start.2
  211.2 228.6 %reduce-scatter.5.cloned.1.call-start = ((), (), s32[]{:S(2)}) async-start(), calls=%async_computation.6 | async-start | bytes 14155776 | tf_op jit(solution)/shard_map/reduce_scatter | solution.py:48
  211.4 3.5 copy-start.1
  214.8 2.2 copy-start.3
Sparse Core Ops, SparseCore 0:
  20.3 30.8 all-gather.8
  54.1 71.6 all-gather.12
  127.5 34.7 all-gather.10
  163.9 37.2 all-gather.6
  211.3 75.0 reduce-scatter.2
  290.1 149.6 reduce-scatter.4
where the time goes:
time: 451 us
  waiting for transfers between devices  369 us (82%)
  local copies, waits for them, and re-layouts  25.4 us (6%)
  matrix products  20.7 us (5%)
  between operations  14.2 us (3%)
  blocking collectives  12.9 us (3%)
  other arithmetic  7.91 us (2%)
    reduce_scatter x2, waiting for transfers between devices, own_rows(): lax.psum_scatter(portion(jnp.int32(0), count), axis, scatter_dimension=0,...  215 us
    all_gather x1, waiting for transfers between devices, one_gather(): lines, at, outs = (lax.all_gather(line, axis), 0, [])  70.3 us
    all_gather x1, waiting for transfers between devices, shards(): grads = lax.all_gather(out_grad, 'tp', axis=1, tiled=True)  33.2 us
    all_gather x1, waiting for transfers between devices, stacked_from(): parts = lax.all_gather(parts, axes[k], axis=0, tiled=True)  27.7 us
    all_gather x1, waiting for transfers between devices, shards(): whole = lax.all_gather(tokens, 'tp', axis=1, tiled=True)  21.9 us
    all_gather x1, blocking collectives, stacked_from(): parts = lax.all_gather(parts, axes[k], axis=0, tiled=True)  12.9 us
  transfers between devices with their start and end apart: 6, of which 6 were waited for; matrix products, arithmetic and copies ran while one was open for 9% of the time, Pallas kernels for 0%

commit v1 on v0

--- a/solution.py
+++ b/solution.py
@@ -27,7 +27,13 @@
 def stacked_from(value, axes, turns):
     parts = value[None]
     for k in turns:
-        parts = lax.all_gather(parts, axes[k], axis=0, tiled=True)
+
+        def column_connect(piece_in, row_axis, array_axis):
+            carry_out = jnp.stack([piece_in] * lax.axis_size(row_axis))
+            v_now = lax.all_to_all(carry_out, row_axis, 0, 0)
+            return jnp.concatenate(v_now, array_axis)
+
+        parts = column_connect(parts, axes[k], array_axis=0)
     current = [lax.axis_size(axes[k]) for k in reversed(turns)]
     parts = parts.reshape(*current, *value.shape)
     turned = sorted(range(len(turns)), key=lambda place: turns[len(turns) - 1 - place])

time: 451 us -> 414 us (0.918)
  waiting for transfers between devices: 369 us -> 321 us
    all_gather x1, waiting for transfers between devices: 70.3 us -> 14.1 us  [one_gather(): lines, at, outs = (lax.all_gather(line, axis), 0, [])]
    all_to_all x0 -> x1, waiting for transfers between devices: none -> 36 us  [column_connect(): v_now = lax.all_to_all(carry_out, row_axis, 0, 0)]
    all_gather x1 -> x0, waiting for transfers between devices: 27.7 us -> none  [stacked_from(): parts = lax.all_gather(parts, axes[k], axis=0, tiled=True)]
    all_to_all x0 -> x1, blocking collectives: none -> 14.5 us  [column_connect(): v_now = lax.all_to_all(carry_out, row_axis, 0, 0)]
    all_gather x1 -> x0, blocking collectives: 12.9 us -> none  [stacked_from(): parts = lax.all_gather(parts, axes[k], axis=0, tiled=True)]
  transfers between devices with their start and end apart: 6 -> 6, of which waited for: 6 -> 6; matrix products, arithmetic and copies ran while one was open for 9% -> 10% of each run, Pallas kernels for 0% -> 0%
where the time goes in v1:
time: 414 us; the launch traced here: 413 us
  waiting for transfers between devices  321 us (78%)
  local copies, waits for them, and re-layouts  28.4 us (7%)
  matrix products  21.2 us (5%)
  blocking collectives  14.5 us (4%)
  between operations  13.8 us (3%)
  other arithmetic  8.95 us (2%)
  starting transfers between devices  4.81 us (1%)
    reduce_scatter x2, waiting for transfers between devices, own_rows(): lax.psum_scatter(portion(jnp.int32(0), count), axis, scatter_dimension=0,...  215 us
    all_to_all x1, waiting for transfers between devices, column_connect(): v_now = lax.all_to_all(carry_out, row_axis, 0, 0)  36 us
    all_gather x1, waiting for transfers between devices, shards(): grads = lax.all_gather(out_grad, 'tp', axis=1, tiled=True)  32.9 us
    all_gather x1, waiting for transfers between devices, shards(): whole = lax.all_gather(tokens, 'tp', axis=1, tiled=True)  21.9 us
    all_to_all x1, blocking collectives, column_connect(): v_now = lax.all_to_all(carry_out, row_axis, 0, 0)  14.5 us
    all_gather x1, waiting for transfers between devices, one_gather(): lines, at, outs = (lax.all_gather(line, axis), 0, [])  14.1 us
  transfers between devices with their start and end apart: 6, of which 6 were waited for; matrix products, arithmetic and copies ran while one was open for 10% of the time, Pallas kernels for 0%

profile of v1, /device:TPU:0, one launch (start us, length us, event | category | flops | bytes accessed | tf_op | source)
XLA Modules:
  0.0 413.1 jit_solution(3716258025490850368)
XLA Ops:
  7.2 0.0 all-gather.9.cloned.1.call-start
  7.2 1.9 pad_maximum_fusion.1
  9.1 0.0 all-gather.9.cloned.1.call-update
  9.1 0.0 all-gather.7.cloned.1.call-start
  9.1 0.7 all-gather.7.cloned.1.call-update
  9.8 1.1 pad_maximum_fusion.2
  10.9 14.5 %all_to_all.10 = bf16[2,1,128,1024]{3,2,1,0:T(8,128)(2,1)S(1)} all-to-all(bf16[2,1,128,1024]{3,2,1,0:T(8,128)(2,1)S(1)} %pad_maximum_fusion.2), channel_id=1, replica_groups=mesh['fsdp_0'=2,'fsdp_1'=4,'tp'=16] {'fsdp_0'}, dimensions={0} | all-to-all | bytes 1048576 | tf_op jit(solution)/shard_map/all_to_all | solution.py:33
  25.5 1.6 stack.7
  27.1 4.5 %all-to-all-start.1 = ((bf16[4,2,128,1024]{3,2,1,0:T(8,128)(2,1)}), bf16[4,2,128,1024]{3,2,1,0:T(8,128)(2,1)S(1)}, u32[]{:S(2)}, u32[]{:S(2)}) async-start(bf16[4,2,128,1024]{3,2,1,0:T(8,128)(2,1)} %stack.7), calls=%async_computation.1 | async-start | bytes 4194304 | tf_op jit(solution)/shard_map/all_to_all | solution.py:33
  31.5 0.0 all-gather.5.cloned.1.call-start
  31.5 0.7 all-gather.5.cloned.1.call-update
  32.3 0.0 reduce-scatter.3.cloned.1.call-start
  32.3 36.0 %all-to-all-done.1 = bf16[4,2,128,1024]{3,2,1,0:T(8,128)(2,1)S(1)} async-done(((bf16[4,2,128,1024]{3,2,1,0:T(8,128)(2,1)}), bf16[4,2,128,1024]{3,2,1,0:T(8,128)(2,1)S(1)}, u32[]{:S(2)}, u32[]{:S(2)}) %all-to-all-start.1) | async-done | bytes 2097184 | tf_op jit(solution)/shard_map/all_to_all | solution.py:33
  68.3 1.6 copy.16
  69.9 3.9 copy.17
  73.9 14.1 %all-gather.9.cloned.1.call-done = bf16[2097152]{0:T(1024)(128)(2,1)} async-done(((bf16[262144]{0:T(1024)(128)(2,1)}), bf16[2097152]{0:T(1024)(128)(2,1)}) %all-gather.9.cloned.1.call-update) | async-done | bytes 4194320 | tf_op jit(solution)/shard_map/all_gather | solution.py:19
  88.0 5.9 %reshape.26 = bf16[8,262144]{1,0:T(8,128)(2,1)} reshape(bf16[2097152]{0:T(1024)(128)(2,1)} %all-gather.9.cloned.1.call-done) | data formatting | bytes 8388608 | tf_op jit(solution)/shard_map/all_gather | solution.py:19
  93.8 3.9 fusion.6
  97.7 2.3 reshape_reshape.6
  100.0 2.6 reshape_reshape.7
  102.6 21.9 %all-gather.7.cloned.1.call-done = bf16[256,8192]{1,0:T(8,128)(2,1)} async-done(((bf16[256,512]{1,0:T(8,128)(2,1)}), bf16[256,8192]{1,0:T(8,128)(2,1)}) %all-gather.7.cloned.1.call-update) | async-done | bytes 4194320 | tf_op jit(solution)/shard_map/all_gather | solution.py:67
  124.5 0.0 copy-start
  124.5 4.5 %convolution_bitcast_fusion = f32[256,128]{0,1:T(8,128)S(1)} fusion(bf16[8192,128]{1,0:T(8,128)(2,1)} %reshape_reshape.6, bf16[256,8192]{1,0:T(8,128)(2,1)} %all-gather.7.cloned.1.call-done), kind=kOutput, calls=%fused_computation.8 | convolution fusion | flops 536870912 | bytes 6422528 | tf_op jit(solution)/shard_map/dot_general | solution.py:70
  128.9 0.0 copy-done
  128.9 1.6 convolution_bitcast_fusion.1
  130.5 32.9 %all-gather.5.cloned.1.call-done = bf16[256,8192]{1,0:T(8,128)(2,1)} async-done(((bf16[256,512]{1,0:T(8,128)(2,1)}), bf16[256,8192]{1,0:T(8,128)(2,1)}) %all-gather.5.cloned.1.call-update) | async-done | bytes 4194320 | tf_op jit(solution)/shard_map/all_gather | solution.py:68
  163.4 0.0 copy-start.2
  163.4 4.5 %multiply_convert_fusion.1 = (bf16[256,128]{0,1:T(8,128)(2,1)S(1)}, bf16[256,128]{0,1:T(8,128)(2,1)S(1)}) fusion(f32[256,128]{0,1:T(8,128)S(1)} %convolution_bitcast_fusion, f32[256,128]{0,1:T(8,128)S(1)} %convolution_bitcast_fusion.1, bf16[128,8192]{0,1:T(8,128)(2,1)} %bitcast.41, bf16[256,8192]{1,0:T(8,128)(2,1)} %all-gather.5.cloned.1.call-done), kind=kOutput, calls=%fused_computation.16 | convolution fusion | flops 537296896 | bytes 6684672 | tf_op jit(solution)/shard_map/dot_general | solution.py:75
  167.9 0.0 copy-done.2
  167.9 1.2 fusion.7
  169.2 4.5 %convolution_add_fusion = f32[8192,256]{1,0:T(8,128)} fusion(f32[8192,256]{1,0:T(8,128)S(1)} %fusion.7, bf16[8192,128]{1,0:T(8,128)(2,1)S(1)} %reshape_reshape.7, bf16[256,128]{0,1:T(8,128)(2,1)S(1)} %get-tuple-element.21), kind=kOutput, calls=%fused_computation.1 | convolution fusion | flops 538968064 | bytes 18939904 | tf_op jit(solution)/shard_map/dot_general | solution.py:94
  173.6 0.0 reduce-scatter.3.cloned.1.call-update
  173.6 0.2 reduce-scatter.5.cloned.1.call-start
  173.9 0.0 copy-start.1
  173.9 3.2 fusion.1
  177.1 0.2 copy-done.1
  177.3 0.0 copy-start.3
  177.3 0.9 fusion.2
  178.2 1.3 copy-done.3
  179.5 0.9 fusion
  180.4 4.9 %pad_maximum_fusion = f32[8192,384]{0,1:T(8,128)} fusion(f32[8192,128]{0,1:T(8,128)S(1)} %fusion, f32[8192,128]{0,1:T(8,128)S(1)} %fusion.1, f32[8192,128]{0,1:T(8,128)S(1)} %fusion.2), kind=kLoop, calls=%fused_computation | loop fusion | flops 6291456 | bytes 25165824 | tf_op jit(solution)/shard_map/concatenate | solution.py:104
  185.4 0.0 reduce-scatter.5.cloned.1.call-update
  185.4 63.4 %reduce-scatter.3.cloned.1.call-done = f32[512,256]{1,0:T(8,128)} async-done(((f32[8192,256]{1,0:T(8,128)}), f32[512,256]{1,0:T(8,128)}) %reduce-scatter.3.cloned.1.call-update) | async-done | bytes 524304 | tf_op jit(solution)/shard_map/reduce_scatter | solution.py:54
  248.8 1.1 convert_bitcast_fusion
  249.9 0.8 copy.18
  250.7 151.6 %reduce-scatter.5.cloned.1.call-done = f32[1024,384]{0,1:T(8,128)} async-done(((f32[8192,384]{0,1:T(8,128)}), f32[1024,384]{0,1:T(8,128)}) %reduce-scatter.5.cloned.1.call-update) | async-done | bytes 1572880 | tf_op jit(solution)/shard_map/reduce_scatter | solution.py:54
  402.3 2.3 slice_bitcast_fusion
  404.6 1.0 copy.19
  405.5 1.0 copy.20
Async XLA Ops:
  7.2 80.8 %all-gather.9.cloned.1.call-start = ((), (), s32[]{:S(2)}) async-start(), calls=%async_computation.8 | async-start | bytes 4718592 | tf_op jit(solution)/shard_map/all_gather | solution.py:19
  9.1 115.4 %all-gather.7.cloned.1.call-start = ((), (), s32[]{:S(2)}) async-start(), calls=%async_computation.5 | async-start | bytes 4456448 | tf_op jit(solution)/shard_map/all_gather | solution.py:67
  27.1 41.2 %all-to-all-start.1 = ((bf16[4,2,128,1024]{3,2,1,0:T(8,128)(2,1)}), bf16[4,2,128,1024]{3,2,1,0:T(8,128)(2,1)S(1)}, u32[]{:S(2)}, u32[]{:S(2)}) async-start(bf16[4,2,128,1024]{3,2,1,0:T(8,128)(2,1)} %stack.7), calls=%async_computation.1 | async-start | bytes 4194304 | tf_op jit(solution)/shard_map/all_to_all | solution.py:33
  31.5 131.9 %all-gather.5.cloned.1.call-start = ((), (), s32[]{:S(2)}) async-start(), calls=%async_computation.4 | async-start | bytes 4456448 | tf_op jit(solution)/shard_map/all_gather | solution.py:68
  32.3 216.5 %reduce-scatter.3.cloned.1.call-start = ((), (), s32[]{:S(2)}) async-start(), calls=%async_computation.6 | async-start | bytes 8912896 | tf_op jit(solution)/shard_map/reduce_scatter | solution.py:54
  124.5 4.5 %copy-start = (bf16[256,8192]{1,0:T(8,128)(2,1)S(1)}, bf16[256,8192]{1,0:T(8,128)(2,1)}, u32[]{:S(2)}) copy-start(bf16[256,8192]{1,0:T(8,128)(2,1)} %all-gather.7.cloned.1.call-done) | copy-start | bytes 12582916
  163.4 4.5 %copy-start.2 = (bf16[8192,128]{1,0:T(8,128)(2,1)S(1)}, bf16[8192,128]{1,0:T(8,128)(2,1)}, u32[]{:S(2)}) copy-start(bf16[8192,128]{1,0:T(8,128)(2,1)} %reshape_reshape.6) | copy-start | bytes 6291460
  173.6 228.6 %reduce-scatter.5.cloned.1.call-start = ((), (), s32[]{:S(2)}) async-start(), calls=%async_computation.7 | async-start | bytes 14155776 | tf_op jit(solution)/shard_map/reduce_scatter | solution.py:54
  173.9 3.5 copy-start.1
  177.3 2.2 copy-start.3
Sparse Core Ops, SparseCore 0:
  10.9 77.0 all-gather.8
  89.6 34.7 all-gather.6
  126.1 37.2 all-gather.4
  173.8 75.0 reduce-scatter.2
  252.6 149.6 reduce-scatter.4
